TPU v7x, 32 devices: a whole 2x2x4 slice. The times are simulated.
32 devices in a mesh: patch: 16 (over z, y, x), shell: 2 (over core).
Axes of the slice: x: 2, y: 2, z: 4, core: 2. Of those that a mesh axis runs over, the one named last changes fastest.
Arguments:
- velocity: float32 [3, 64, 16, 512], P(None, 'patch', None, 'shell'), may hold values from -4 to 4
- pressure: float32 [4, 32, 8, 256], P(None, 'patch', None, 'shell'), may hold values from -6 to 6
- force: float32 [3, 64, 16, 512], P(None, 'patch', None, 'shell'), may hold values from -6 to 6
- viscosity: float32 [32, 8, 256], P('patch', None, 'shell'), may hold values from 0.1 to 10
- element_stiffness: float32 [81, 81], replicated, as said below
- element_divergence: float32 [4, 81], replicated, may hold values from -0.625 to 0.625
Outputs:
- solution: float32 [3, 64, 16, 512], P(None, 'patch', None, 'shell')
- new_pressure: float32 [4, 32, 8, 256], P(None, 'patch', None, 'shell')
Inputs may be any that keep to these rules, and one draw needn't show every extreme that they name: `element_stiffness`: symmetric and positive definite.
All inputs are finite; a program needn't handle non-finite values.
Results may differ from a plain program's by a relative error of at most 0.0003.
Values sent between devices are 32-bit elements; how exact they have to be, the bound alone decides.
A program may use at most 64 MiB of HBM per device.

v0:
```python
import jax
import jax.numpy as jnp
from jax import lax
from jax.sharding import PartitionSpec as P

ITERS = 2


relaxation = 1.0


def from_behind(value, axis, steps):
    count = lax.axis_size(axis)
    pairs = [(source, (source + steps) % count) for source in range(count)]
    return lax.ppermute(value, axis, pairs)


def passed_along(block, axis, distance):
    devices = range(lax.axis_size(axis))
    route = [(i - distance, i) for i in devices if i - distance in devices]
    return lax.ppermute(block, axis, route)


def selectors(elem_count):
    node_index = lax.broadcasted_iota(jnp.int32, (3, 2 * elem_count + 1, elem_count), 1)
    elem_index = lax.broadcasted_iota(jnp.int32, (3, 2 * elem_count + 1, elem_count), 2)
    offset = lax.broadcasted_iota(jnp.int32, (3, 2 * elem_count + 1, elem_count), 0)
    return (node_index == 2 * elem_index + offset).astype(jnp.float32)


def element_values(extended, elem_a, elem_b, elem_r):
    sel_a = selectors(elem_a)
    sel_b = selectors(elem_b)
    sel_r = selectors(elem_r)
    radial = jnp.einsum(
        "xpqn,cnk->xpqck",
        extended,
        sel_r,
        precision=lax.Precision.HIGHEST,
        preferred_element_type=jnp.float32,
    )
    middle = jnp.einsum(
        "xpqck,bqj->xpbcjk",
        radial,
        sel_b,
        precision=lax.Precision.HIGHEST,
        preferred_element_type=jnp.float32,
    )
    outer = jnp.einsum(
        "xpbcjk,api->xabcijk",
        middle,
        sel_a,
        precision=lax.Precision.HIGHEST,
        preferred_element_type=jnp.float32,
    )
    return outer.reshape(81, elem_a * elem_b * elem_r)


def assemble(element_terms, elem_a, elem_b, elem_r):
    sel_a = selectors(elem_a)
    sel_b = selectors(elem_b)
    sel_r = selectors(elem_r)
    split_terms = element_terms.reshape(3, 3, 3, 3, elem_a, elem_b, elem_r)
    radial = jnp.einsum(
        "xabcijk,cnk->xabijn",
        split_terms,
        sel_r,
        precision=lax.Precision.HIGHEST,
        preferred_element_type=jnp.float32,
    )
    middle = jnp.einsum(
        "xabijn,bqj->xaiqn",
        radial,
        sel_b,
        precision=lax.Precision.HIGHEST,
        preferred_element_type=jnp.float32,
    )
    return jnp.einsum(
        "xaiqn,api->xpqn",
        middle,
        sel_a,
        precision=lax.Precision.HIGHEST,
        preferred_element_type=jnp.float32,
    )


def element_terms_of(values, stiffness, divergence_map, visc_flat, pressure_flat):
    element_terms = (
        jnp.dot(
            stiffness, values, precision=lax.Precision.HIGHEST, preferred_element_type=jnp.float32
        )
        * visc_flat[None, :]
    )
    if pressure_flat is not None:
        element_terms = element_terms + jnp.dot(
            divergence_map.T,
            pressure_flat,
            precision=lax.Precision.HIGHEST,
            preferred_element_type=jnp.float32,
        )
    return element_terms


def widen_field(nodal_field):
    next_plane = from_behind(nodal_field[:, :1], "patch", -1)
    widened = jnp.concatenate([nodal_field, next_plane], axis=1)
    top_plane = passed_along(widened[:, :, :, :1], "shell", -1)
    widened = jnp.concatenate([widened, top_plane], axis=3)
    zero_plane = jnp.zeros_like(widened[:, :, :1])
    return jnp.concatenate([widened, zero_plane], axis=2)


def fold_planes(summed, nodes_a, nodes_b, nodes_r):
    interior = summed[:, :, :nodes_b]
    from_below = passed_along(interior[:, :, :, nodes_r:], "shell", 1)
    interior = interior[:, :, :, :nodes_r]
    interior = jnp.concatenate([interior[:, :, :, :1] + from_below, interior[:, :, :, 1:]], axis=3)
    from_before = from_behind(interior[:, nodes_a:], "patch", 1)
    owned_part = interior[:, :nodes_a]
    return jnp.concatenate([owned_part[:, :1] + from_before, owned_part[:, 1:]], axis=1)


def per_device(velocity, pressure, force, viscosity, element_stiffness, element_divergence):
    elem_a, elem_b, elem_r = viscosity.shape
    elements = elem_a * elem_b * elem_r
    nodes_a, nodes_b, nodes_r = (velocity.shape[1], velocity.shape[2], velocity.shape[3])
    visc_flat = viscosity.reshape(elements)
    pressure_flat = pressure.reshape(4, elements)
    solution = velocity
    extended = widen_field(solution)
    values = element_values(extended, elem_a, elem_b, elem_r)
    for iteration in range(ITERS):
        terms_u = element_terms_of(
            values, element_stiffness, element_divergence, visc_flat, pressure_flat
        )
        image_u = fold_planes(assemble(terms_u, elem_a, elem_b, elem_r), nodes_a, nodes_b, nodes_r)
        residual = force - image_u
        local_norm = jnp.sum(residual * residual)
        norm_sq = lax.psum(local_norm, ("patch", "shell"))
        residual_ext = widen_field(residual)
        residual_values = element_values(residual_ext, elem_a, elem_b, elem_r)
        terms_r = element_terms_of(
            residual_values, element_stiffness, element_divergence, visc_flat, None
        )
        image_r = fold_planes(assemble(terms_r, elem_a, elem_b, elem_r), nodes_a, nodes_b, nodes_r)
        local_curv = jnp.sum(residual * image_r)
        curv_sum = lax.psum(local_curv, ("patch", "shell"))
        step_size = norm_sq / curv_sum
        solution = solution + step_size * residual
        extended = extended + step_size * residual_ext
        values = element_values(extended, elem_a, elem_b, elem_r)
        divergence = jnp.dot(
            element_divergence,
            values,
            precision=lax.Precision.HIGHEST,
            preferred_element_type=jnp.float32,
        )
        pressure_flat = pressure_flat + relaxation * divergence / visc_flat[None, :]
    return (solution, pressure_flat.reshape(4, elem_a, elem_b, elem_r))


def solution(mesh):
    return jax.shard_map(
        per_device,
        mesh=mesh,
        in_specs=(
            P(None, "patch", None, "shell"),
            P(None, "patch", None, "shell"),
            P(None, "patch", None, "shell"),
            P("patch", None, "shell"),
            P(),
            P(),
        ),
        out_specs=(P(None, "patch", None, "shell"), P(None, "patch", None, "shell")),
        check_vma=False,
    )
```

profile of v0, /device:TPU:0, one launch (start us, length us, event | category | flops | bytes accessed | tf_op | source)
XLA Modules:
  0.0 182.1 jit_solution(3848757845363828760)
XLA Ops:
  1.5 7.0 %collective-permute-start = (f32[3,1,16,256]{3,1,2,0:T(1,128)S(1)}, f32[3,1,16,256]{3,1,2,0:T(1,128)S(1)}, u32[]{:S(2)}, u32[]{:S(2)}) collective-permute-start(f32[3,1,16,256]{3,1,2,0:T(1,128)S(1)} %copy.14), channel_id=1, source_target_pairs={{0,30},{2,0},{4,2},{6,4},{8,6},{10,8},{12,10},{14,12},{16,14},{18,... | collective-permute-start | bytes 147464 | tf_op jit(solution)/shard_map/ppermute | solution.py:15
  8.5 1.1 copy.19
  10.3 1.3 collective-permute-start.1
  11.6 2.0 %collective-permute-done.1 = f32[3,5,16,1]{3,1,2,0:T(8,128)S(1)} collective-permute-done((f32[3,5,16,1]{3,1,2,0:T(8,128)S(1)}, f32[3,5,16,1]{3,1,2,0:T(8,128)S(1)}, u32[]{:S(2)}, u32[]{:S(2)}) %collective-permute-start.1) | collective-permute-done | bytes 992 | tf_op jit(solution)/shard_map/ppermute | solution.py:21
  19.6 0.9 convolution_bitcast_fusion.16
  20.5 2.1 %collective-permute-start.2 = (f32[3,5,16,1]{3,1,2,0:T(8,128)S(1)}, f32[3,5,16,1]{3,1,2,0:T(8,128)S(1)}, u32[]{:S(2)}, u32[]{:S(2)}) collective-permute-start(f32[3,5,16,1]{3,1,2,0:T(8,128)S(1)} %slice.157), channel_id=1, source_target_pairs={{0,1},{2,3},{4,5},{6,7},{8,9},{10,11},{12,13},{14,15},{16,17},{18,... | collective-permute-start | bytes 2888 | tf_op jit(solution)/shard_map/ppermute | solution.py:21
  22.8 0.9 collective-permute-done.2
  23.9 8.3 %collective-permute-done.3 = f32[3,1,16,256]{3,1,2,0:T(1,128)S(1)} collective-permute-done((f32[3,1,16,256]{3,1,2,0:T(1,128)S(1)}, f32[3,1,16,256]{3,1,2,0:T(1,128)S(1)}, u32[]{:S(2)}, u32[]{:S(2)}) %collective-permute-start.3) | collective-permute-done | bytes 49184 | tf_op jit(solution)/shard_map/ppermute | solution.py:15
  32.7 1.8 collective-permute-start.4
  34.5 2.4 %collective-permute-done.4 = f32[3,1,16,256]{3,1,2,0:T(1,128)S(1)} collective-permute-done((f32[3,1,16,256]{3,1,2,0:T(1,128)S(1)}, f32[3,1,16,256]{3,1,2,0:T(1,128)S(1)}, u32[]{:S(2)}, u32[]{:S(2)}) %collective-permute-start.4) | collective-permute-done | bytes 49184 | tf_op jit(solution)/shard_map/ppermute | solution.py:15
  36.9 1.5 collective-permute-start.5
  38.4 1.9 %collective-permute-done.5 = f32[3,5,16,1]{3,1,2,0:T(8,128)S(1)} collective-permute-done((f32[3,5,16,1]{3,1,2,0:T(8,128)S(1)}, f32[3,5,16,1]{3,1,2,0:T(8,128)S(1)}, u32[]{:S(2)}, u32[]{:S(2)}) %collective-permute-start.5) | collective-permute-done | bytes 992 | tf_op jit(solution)/shard_map/ppermute | solution.py:21
  41.6 0.8 convolution_bitcast_fusion.3
  44.8 0.9 convolution_bitcast_fusion.15
  45.7 2.1 %collective-permute-start.6 = (f32[3,5,16,1]{3,1,2,0:T(8,128)S(1)}, f32[3,5,16,1]{3,1,2,0:T(8,128)S(1)}, u32[]{:S(2)}, u32[]{:S(2)}) collective-permute-start(f32[3,5,16,1]{3,1,2,0:T(8,128)S(1)} %slice.161), channel_id=1, source_target_pairs={{0,1},{2,3},{4,5},{6,7},{8,9},{10,11},{12,13},{14,15},{16,17},{18,... | collective-permute-start | bytes 2888 | tf_op jit(solution)/shard_map/ppermute | solution.py:21
  47.9 0.9 collective-permute-done.6
  49.1 7.7 %collective-permute-done.7 = f32[3,1,16,256]{3,1,2,0:T(1,128)S(1)} collective-permute-done((f32[3,1,16,256]{3,1,2,0:T(1,128)S(1)}, f32[3,1,16,256]{3,1,2,0:T(1,128)S(1)}, u32[]{:S(2)}, u32[]{:S(2)}) %collective-permute-start.7) | collective-permute-done | bytes 49184 | tf_op jit(solution)/shard_map/ppermute | solution.py:15
  57.7 37.3 %all-reduce.4 = (f32[]{:T(128)}, f32[]{:T(128)}) all-reduce(f32[]{:T(128)} %get-tuple-element.9, f32[]{:T(128)} %get-tuple-element.8), channel_id=1, replica_groups=mesh['patch'=16,'shell'=2] {'patch','shell'}, use_global_device_ids=true, to_apply=%region_1.0 | all-reduce | flops 2 | bytes 16 | tf_op jit(solution)/shard_map/psum | solution.py:139
  102.3 0.9 convolution_bitcast_fusion.14
  103.2 1.3 collective-permute-start.8
  104.7 0.9 collective-permute-done.8
  105.8 2.3 %collective-permute-start.9 = (f32[3,1,16,256]{3,1,2,0:T(1,128)S(1)}, f32[3,1,16,256]{3,1,2,0:T(1,128)S(1)}, u32[]{:S(2)}, u32[]{:S(2)}) collective-permute-start(f32[3,1,16,256]{3,1,2,0:T(1,128)S(1)} %pad_maximum_fusion.4), channel_id=1, source_target_pairs={{0,2},{2,4},{4,6},{6,8},{8,10},{10,12},{12,14},{14,16},{16,18},{18... | collective-permute-start | bytes 147464 | tf_op jit(solution)/shard_map/ppermute | solution.py:15
  108.1 5.4 %collective-permute-done.9 = f32[3,1,16,256]{3,1,2,0:T(1,128)S(1)} collective-permute-done((f32[3,1,16,256]{3,1,2,0:T(1,128)S(1)}, f32[3,1,16,256]{3,1,2,0:T(1,128)S(1)}, u32[]{:S(2)}, u32[]{:S(2)}) %collective-permute-start.9) | collective-permute-done | bytes 49184 | tf_op jit(solution)/shard_map/ppermute | solution.py:15
  114.3 3.9 %collective-permute-done.10 = f32[3,1,16,256]{3,1,2,0:T(1,128)S(1)} collective-permute-done((f32[3,1,16,256]{3,1,2,0:T(1,128)S(1)}, f32[3,1,16,256]{3,1,2,0:T(1,128)S(1)}, u32[]{:S(2)}, u32[]{:S(2)}) %collective-permute-start.10) | collective-permute-done | bytes 49184 | tf_op jit(solution)/shard_map/ppermute | solution.py:15
  118.2 1.6 collective-permute-start.11
  119.8 1.8 collective-permute-done.11
  122.9 0.8 convolution_bitcast_fusion.1
  126.1 0.9 convolution_bitcast_fusion.13
  127.0 2.1 %collective-permute-start.12 = (f32[3,5,16,1]{3,1,2,0:T(8,128)S(1)}, f32[3,5,16,1]{3,1,2,0:T(8,128)S(1)}, u32[]{:S(2)}, u32[]{:S(2)}) collective-permute-start(f32[3,5,16,1]{3,1,2,0:T(8,128)S(1)} %slice.168), channel_id=1, source_target_pairs={{0,1},{2,3},{4,5},{6,7},{8,9},{10,11},{12,13},{14,15},{16,17},{18,... | collective-permute-start | bytes 2888 | tf_op jit(solution)/shard_map/ppermute | solution.py:21
  129.2 0.9 collective-permute-done.12
  130.4 7.7 %collective-permute-done.13 = f32[3,1,16,256]{3,1,2,0:T(1,128)S(1)} collective-permute-done((f32[3,1,16,256]{3,1,2,0:T(1,128)S(1)}, f32[3,1,16,256]{3,1,2,0:T(1,128)S(1)}, u32[]{:S(2)}, u32[]{:S(2)}) %collective-permute-start.13) | collective-permute-done | bytes 49184 | tf_op jit(solution)/shard_map/ppermute | solution.py:15
  139.0 37.1 %all-reduce.3 = (f32[]{:T(128)}, f32[]{:T(128)}) all-reduce(f32[]{:T(128)} %get-tuple-element.7, f32[]{:T(128)} %get-tuple-element.6), channel_id=1, replica_groups=mesh['patch'=16,'shell'=2] {'patch','shell'}, use_global_device_ids=true, to_apply=%region_5.0 | all-reduce | flops 2 | bytes 16 | tf_op jit(solution)/shard_map/psum | solution.py:139
  (107 shorter events, 30.2 us)
Async XLA Ops:
  0.6 15.4 %copy-start = (f32[81,81]{1,0:T(8,128)S(1)}, f32[81,81]{1,0:T(8,128)}, u32[]{:S(2)}) copy-start(f32[81,81]{1,0:T(8,128)} %param.10) | copy-start | bytes 78736
  0.6 0.8 slice-start
  1.5 8.8 %collective-permute-start = (f32[3,1,16,256]{3,1,2,0:T(1,128)S(1)}, f32[3,1,16,256]{3,1,2,0:T(1,128)S(1)}, u32[]{:S(2)}, u32[]{:S(2)}) collective-permute-start(f32[3,1,16,256]{3,1,2,0:T(1,128)S(1)} %copy.14), channel_id=1, source_target_pairs={{0,30},{2,0},{4,2},{6,4},{8,6},{10,8},{12,10},{14,12},{16,14},{18,... | collective-permute-start | bytes 147464 | tf_op jit(solution)/shard_map/ppermute | solution.py:15
  10.3 3.3 %collective-permute-start.1 = (f32[3,5,16,1]{3,1,2,0:T(8,128)S(1)}, f32[3,5,16,1]{3,1,2,0:T(8,128)S(1)}, u32[]{:S(2)}, u32[]{:S(2)}) collective-permute-start(f32[3,5,16,1]{3,1,2,0:T(8,128)S(1)} %pad_maximum_fusion.2), channel_id=1, source_target_pairs={{1,0},{3,2},{5,4},{7,6},{9,8},{11,10},{13,12},{15,14},{17,16},{19,... | collective-permute-start | bytes 2888 | tf_op jit(solution)/shard_map/ppermute | solution.py:21
  15.9 0.7 copy-start.3
  16.6 0.8 copy-start.4
  16.6 0.8 copy-start.5
  20.5 3.1 %collective-permute-start.2 = (f32[3,5,16,1]{3,1,2,0:T(8,128)S(1)}, f32[3,5,16,1]{3,1,2,0:T(8,128)S(1)}, u32[]{:S(2)}, u32[]{:S(2)}) collective-permute-start(f32[3,5,16,1]{3,1,2,0:T(8,128)S(1)} %slice.157), channel_id=1, source_target_pairs={{0,1},{2,3},{4,5},{6,7},{8,9},{10,11},{12,13},{14,15},{16,17},{18,... | collective-permute-start | bytes 2888 | tf_op jit(solution)/shard_map/ppermute | solution.py:21
  23.8 8.6 %copy-start.2 = (f32[3,4,16,256]{3,2,1,0:T(8,128)S(1)}, f32[3,4,16,256]{3,2,1,0:T(8,128)}, u32[]{:S(2)}) copy-start(f32[3,4,16,256]{3,2,1,0:T(8,128)} %param.8) | copy-start | bytes 589828
  23.9 8.4 %collective-permute-start.3 = (f32[3,1,16,256]{3,1,2,0:T(1,128)S(1)}, f32[3,1,16,256]{3,1,2,0:T(1,128)S(1)}, u32[]{:S(2)}, u32[]{:S(2)}) collective-permute-start(f32[3,1,16,256]{3,1,2,0:T(1,128)S(1)} %pad_maximum_fusion.6), channel_id=1, source_target_pairs={{0,2},{2,4},{4,6},{6,8},{8,10},{10,12},{12,14},{14,16},{16,18},{18... | collective-permute-start | bytes 147464 | tf_op jit(solution)/shard_map/ppermute | solution.py:15
  32.7 4.1 %collective-permute-start.4 = (f32[3,1,16,256]{3,1,2,0:T(1,128)S(1)}, f32[3,1,16,256]{3,1,2,0:T(1,128)S(1)}, u32[]{:S(2)}, u32[]{:S(2)}) collective-permute-start(f32[3,1,16,256]{3,1,2,0:T(1,128)S(1)} %slice.159), channel_id=1, source_target_pairs={{0,30},{2,0},{4,2},{6,4},{8,6},{10,8},{12,10},{14,12},{16,14},{18,... | collective-permute-start | bytes 147464 | tf_op jit(solution)/shard_map/ppermute | solution.py:15
  36.9 3.3 %collective-permute-start.5 = (f32[3,5,16,1]{3,1,2,0:T(8,128)S(1)}, f32[3,5,16,1]{3,1,2,0:T(8,128)S(1)}, u32[]{:S(2)}, u32[]{:S(2)}) collective-permute-start(f32[3,5,16,1]{3,1,2,0:T(8,128)S(1)} %pad_maximum_fusion.1), channel_id=1, source_target_pairs={{1,0},{3,2},{5,4},{7,6},{9,8},{11,10},{13,12},{15,14},{17,16},{19,... | collective-permute-start | bytes 2888 | tf_op jit(solution)/shard_map/ppermute | solution.py:21
  45.7 3.1 %collective-permute-start.6 = (f32[3,5,16,1]{3,1,2,0:T(8,128)S(1)}, f32[3,5,16,1]{3,1,2,0:T(8,128)S(1)}, u32[]{:S(2)}, u32[]{:S(2)}) collective-permute-start(f32[3,5,16,1]{3,1,2,0:T(8,128)S(1)} %slice.161), channel_id=1, source_target_pairs={{0,1},{2,3},{4,5},{6,7},{8,9},{10,11},{12,13},{14,15},{16,17},{18,... | collective-permute-start | bytes 2888 | tf_op jit(solution)/shard_map/ppermute | solution.py:21
  49.0 7.7 %collective-permute-start.7 = (f32[3,1,16,256]{3,1,2,0:T(1,128)S(1)}, f32[3,1,16,256]{3,1,2,0:T(1,128)S(1)}, u32[]{:S(2)}, u32[]{:S(2)}) collective-permute-start(f32[3,1,16,256]{3,1,2,0:T(1,128)S(1)} %pad_maximum_fusion.5), channel_id=1, source_target_pairs={{0,2},{2,4},{4,6},{6,8},{8,10},{10,12},{12,14},{14,16},{16,18},{18... | collective-permute-start | bytes 147464 | tf_op jit(solution)/shard_map/ppermute | solution.py:15
  103.2 2.4 %collective-permute-start.8 = (f32[3,5,16,1]{3,1,2,0:T(8,128)S(1)}, f32[3,5,16,1]{3,1,2,0:T(8,128)S(1)}, u32[]{:S(2)}, u32[]{:S(2)}) collective-permute-start(f32[3,5,16,1]{3,1,2,0:T(8,128)S(1)} %slice.164), channel_id=1, source_target_pairs={{0,1},{2,3},{4,5},{6,7},{8,9},{10,11},{12,13},{14,15},{16,17},{18,... | collective-permute-start | bytes 2888 | tf_op jit(solution)/shard_map/ppermute | solution.py:21
  105.8 7.7 %collective-permute-start.9 = (f32[3,1,16,256]{3,1,2,0:T(1,128)S(1)}, f32[3,1,16,256]{3,1,2,0:T(1,128)S(1)}, u32[]{:S(2)}, u32[]{:S(2)}) collective-permute-start(f32[3,1,16,256]{3,1,2,0:T(1,128)S(1)} %pad_maximum_fusion.4), channel_id=1, source_target_pairs={{0,2},{2,4},{4,6},{6,8},{8,10},{10,12},{12,14},{14,16},{16,18},{18... | collective-permute-start | bytes 147464 | tf_op jit(solution)/shard_map/ppermute | solution.py:15
  114.0 4.1 %collective-permute-start.10 = (f32[3,1,16,256]{3,1,2,0:T(1,128)S(1)}, f32[3,1,16,256]{3,1,2,0:T(1,128)S(1)}, u32[]{:S(2)}, u32[]{:S(2)}) collective-permute-start(f32[3,1,16,256]{3,1,2,0:T(1,128)S(1)} %slice.166), channel_id=1, source_target_pairs={{0,30},{2,0},{4,2},{6,4},{8,6},{10,8},{12,10},{14,12},{16,14},{18,... | collective-permute-start | bytes 147464 | tf_op jit(solution)/shard_map/ppermute | solution.py:15
  118.2 3.3 %collective-permute-start.11 = (f32[3,5,16,1]{3,1,2,0:T(8,128)S(1)}, f32[3,5,16,1]{3,1,2,0:T(8,128)S(1)}, u32[]{:S(2)}, u32[]{:S(2)}) collective-permute-start(f32[3,5,16,1]{3,1,2,0:T(8,128)S(1)} %pad_maximum_fusion), channel_id=1, source_target_pairs={{1,0},{3,2},{5,4},{7,6},{9,8},{11,10},{13,12},{15,14},{17,16},{19,... | collective-permute-start | bytes 2888 | tf_op jit(solution)/shard_map/ppermute | solution.py:21
  127.0 3.1 %collective-permute-start.12 = (f32[3,5,16,1]{3,1,2,0:T(8,128)S(1)}, f32[3,5,16,1]{3,1,2,0:T(8,128)S(1)}, u32[]{:S(2)}, u32[]{:S(2)}) collective-permute-start(f32[3,5,16,1]{3,1,2,0:T(8,128)S(1)} %slice.168), channel_id=1, source_target_pairs={{0,1},{2,3},{4,5},{6,7},{8,9},{10,11},{12,13},{14,15},{16,17},{18,... | collective-permute-start | bytes 2888 | tf_op jit(solution)/shard_map/ppermute | solution.py:21
  130.3 7.7 %collective-permute-start.13 = (f32[3,1,16,256]{3,1,2,0:T(1,128)S(1)}, f32[3,1,16,256]{3,1,2,0:T(1,128)S(1)}, u32[]{:S(2)}, u32[]{:S(2)}) collective-permute-start(f32[3,1,16,256]{3,1,2,0:T(1,128)S(1)} %pad_maximum_fusion.3), channel_id=1, source_target_pairs={{0,2},{2,4},{4,6},{6,8},{8,10},{10,12},{12,14},{14,16},{16,18},{18... | collective-permute-start | bytes 147464 | tf_op jit(solution)/shard_map/ppermute | solution.py:15
  138.2 39.3 %copy-start.1 = (f32[3,4,16,256]{3,2,1,0:T(8,128)S(1)}, f32[3,4,16,256]{3,2,1,0:T(8,128)}, u32[]{:S(2)}) copy-start(f32[3,4,16,256]{3,2,1,0:T(8,128)} %param.6) | copy-start | bytes 589828
where the time goes:
time: 184 us; the launch traced here: 182 us
  blocking collectives  74.4 us (40%)
  waiting for transfers between devices  45.1 us (25%)
  matrix products  24.4 us (13%)
  starting transfers between devices  23.3 us (13%)
  local copies, waits for them, and re-layouts  6.08 us (3%)
  other arithmetic  4.76 us (3%)
  between operations  4.05 us (2%)
    psum x2, blocking collectives, per_device(): norm_sq = lax.psum(local_norm, ('patch', 'shell'))  74.4 us
    ppermute x7, waiting for transfers between devices, from_behind(): return lax.ppermute(value, axis, pairs)  36 us
    ppermute x7, starting transfers between devices, passed_along(): return lax.ppermute(block, axis, route)  11.8 us
    ppermute x7, starting transfers between devices, from_behind(): return lax.ppermute(value, axis, pairs)  11.6 us
    ppermute x7, waiting for transfers between devices, passed_along(): return lax.ppermute(block, axis, route)  9.13 us
    dot_general x5, matrix products, element_values(): jnp.einsum('xpbcjk,api->xabcijk', middle, sel_a, precision=lax.Precision....  4.06 us
    dot_general x5, matrix products, element_values(): jnp.einsum('xpqn,cnk->xpqck', extended, sel_r, precision=lax.Precision.HI...  3.92 us
    unnamed x23, local copies, waits for them, and re-layouts  3.69 us
  transfers between devices with their start and end apart: 14, of which 14 were waited for; matrix products, arithmetic and copies ran while one was open for 1% of the time, Pallas kernels for 0%

commit v1 on v0

v1 whole, which is shorter than its diff:
```python
import functools

import jax
import jax.numpy as jnp
import numpy as np
from jax import lax
from jax.experimental import pallas as pl
from jax.experimental.pallas import tpu as pltpu
from jax.sharding import PartitionSpec as P

ITERS = 2
MESH = pl.DeviceIdType.MESH
SLOTS = 16
F32 = jnp.float32
BF16 = jnp.bfloat16


def unknown_map():
    rows = np.zeros((9 * SLOTS, 81), np.float32)
    for x in range(3):
        for a in range(3):
            for b in range(3):
                for c in range(3):
                    rows[(b * 3 + a) * SLOTS + c * 3 + x, x * 27 + a * 9 + b * 3 + c] = 1.0
    return rows


def dot(x, y, contract=((1,), (0,))):
    return lax.dot_general(x, y, (contract, ((), ())), preferred_element_type=F32)


def split2(x):
    hi = x.astype(BF16)
    return hi, (x - hi.astype(F32)).astype(BF16)


def exact_dot(x, perm):
    hi, mid = split2(x)
    lo = (x - hi.astype(F32) - mid.astype(F32)).astype(BF16)
    return dot(hi, perm) + dot(mid, perm) + dot(lo, perm)


def kernel(
    dims,
    v_ref, p_ref, f_ref, visc_ref, stiff_ref, div_ref, map_ref,
    sol_ref, pout_ref,
    fld, fhi, flo, out, out2, pq, bvals,
    vplane, vcol, vcol_in, vdiag_in,
    col_out, col_in, plane_out, plane_in, gcol_out, gcol_in, sums,
    bar_send, bar_recv, col_send, col_recv, pl_send, pl_recv, ar_send, ar_recv,
):
    n_patch, n_shell, ea, eb, na, nb, lanes = dims
    n_dev = n_patch * n_shell
    planes = na + 1
    block = 3 * nb
    owned = na * block
    rows = planes * block
    width = vcol.shape[1]
    stride = planes * SLOTS
    patch = lax.axis_index("patch")
    shell = lax.axis_index("shell")
    after = lax.rem(patch + 1, n_patch)
    before = lax.rem(patch + n_patch - 1, n_patch)
    has_above = shell < n_shell - 1
    has_below = shell > 0
    above = jnp.minimum(shell + 1, n_shell - 1)
    below = jnp.maximum(shell - 1, 0)

    def remote(src, dst, send, recv, to_patch, to_shell):
        return pltpu.make_async_remote_copy(
            src_ref=src, dst_ref=dst, send_sem=send, recv_sem=recv,
            device_id={"patch": to_patch, "shell": to_shell}, device_id_type=MESH,
        )

    plane_copy = remote(v_ref.at[:, 0], vplane, bar_send.at[0], bar_recv.at[0], before, shell)
    plane_copy.start()
    head = jnp.concatenate(
        [v_ref[x, a, :, :lanes] for a in range(na) for x in range(3)]
        + [jnp.zeros((width - owned, lanes), F32)], axis=0)
    vcol[...] = jnp.transpose(head)[:8]
    col_copy = remote(vcol, vcol_in, bar_send.at[1], bar_recv.at[1], patch, below)
    diag_copy = remote(vcol, vdiag_in, bar_send.at[2], bar_recv.at[2], before, below)

    @pl.when(has_below)
    def _():
        col_copy.start()
        diag_copy.start()

    row_map = map_ref[...].astype(BF16)
    a_hi, a_lo = split2(stiff_ref[...])
    div = jnp.concatenate([div_ref[...], jnp.zeros((4, 81), F32)], axis=0)
    b_hi = div.astype(BF16).astype(F32)
    b_lo = (div - b_hi).astype(BF16).astype(F32)

    def both_sides(mat):
        return dot(dot(row_map, mat).astype(BF16), row_map, ((1,), (1,)))

    def right_side(mat):
        return dot(mat.astype(BF16), row_map, ((1,), (1,)))

    apply_hi = jnp.concatenate([both_sides(a_hi), right_side(b_hi)], axis=0).astype(BF16)
    apply_lo = jnp.concatenate([both_sides(a_lo), right_side(b_lo)], axis=0).astype(BF16)
    apply_all = jnp.concatenate([apply_hi, apply_lo], axis=0)
    b_stack = jnp.concatenate([b_hi, b_lo, b_hi, jnp.zeros((8, 81), F32)], axis=0).astype(BF16)
    back = dot(row_map, b_stack, ((1,), (1,))).astype(BF16)
    m_rows = 9 * SLOTS
    span = 3 * SLOTS

    r_i = lax.broadcasted_iota(jnp.int32, (2 * lanes, 2 * lanes), 0)
    c_i = lax.broadcasted_iota(jnp.int32, (2 * lanes, 2 * lanes), 1)
    unzip = (r_i == jnp.where(c_i < lanes, 2 * c_i, 2 * c_i - 2 * lanes + 1)).astype(BF16)
    rezip = (c_i == jnp.where(r_i < lanes, 2 * r_i, 2 * r_i - 2 * lanes + 1)).astype(BF16)

    fld[...] = jnp.zeros_like(fld)
    pq[...] = jnp.zeros_like(pq)
    for i in range(ea):
        for q in range(4):
            pq[pl.ds(i * eb * 8 + q, eb, stride=8), :] = p_ref[q, i]
    inv_visc = [1.0 / visc_ref[i] for i in range(ea)]
    visc = [visc_ref[i] for i in range(ea)]

    f_n = exact_dot(jnp.concatenate(
        [f_ref[x, a] for a in range(na) for x in range(3)], axis=0), unzip)
    zero_plane = jnp.zeros((block, lanes), F32)
    f_e = jnp.concatenate([f_n[:, :lanes], zero_plane], axis=0)
    f_o = jnp.concatenate([f_n[:, lanes:], zero_plane], axis=0)
    v_own = exact_dot(jnp.concatenate(
        [v_ref[x, a] for a in range(na) for x in range(3)], axis=0), unzip)

    lane_n = lax.broadcasted_iota(jnp.int32, (rows, lanes), 1)
    col_lane = lax.broadcasted_iota(jnp.int32, (1, width), 1)

    def column(row):
        return jnp.transpose(jnp.broadcast_to(row, (lanes, width)))[:rows]

    def put(even, odd, ghost):
        shifted = pltpu.roll(jnp.where(lane_n == 0, column(ghost), even), lanes - 1, 1)
        for a in range(planes):
            for x in range(3):
                at = (a * 3 + x) * nb
                for c, part in ((0, even), (1, odd), (2, shifted)):
                    fld[pl.ds(a * SLOTS + c * 3 + x, nb, stride=stride), :] = part[at:at + nb]
        hi, lo = split2(fld[...])
        fhi[...] = hi
        flo[...] = lo

    def gathered(ref, j):
        parts = []
        for i in range(ea):
            parts.append(jnp.concatenate(
                [ref[(2 * j + b) * stride + 2 * i * SLOTS:(2 * j + b) * stride + 2 * i * SLOTS + span]
                 for b in range(3)], axis=0))
        return jnp.concatenate(parts, axis=1)

    def back_apply(pieces):
        packed = []
        for w in pieces:
            hi = w.astype(BF16).astype(F32)
            packed.append(jnp.concatenate([hi, hi, w - hi, jnp.zeros_like(w)], axis=0))
        return dot(back, jnp.concatenate(packed, axis=1).astype(BF16))

    def add_to(ref, terms, i, j):
        for b in range(3):
            at = (2 * j + b) * stride + 2 * i * SLOTS
            ref[at:at + span] = ref[at:at + span] + terms[b * span:(b + 1) * span]

    def operator(mode, slot):
        if mode != "last":
            out[...] = jnp.zeros_like(out)
        if mode == "first":
            out2[...] = jnp.zeros_like(out2)
        energy = jnp.zeros((8, lanes), F32)
        for j in range(eb):
            hi = dot(apply_all, gathered(fhi, j))
            full = hi[:m_rows + 8] + hi[m_rows + 8:] + dot(apply_hi, gathered(flo, j))
            scaled = []
            for i in range(ea):
                part = full[:, i * lanes:(i + 1) * lanes]
                at = (i * eb + j) * 8
                bv = part[m_rows:]
                bvals[slot, at:at + 8] = bv
                scaled.append(bv * inv_visc[i][j:j + 1])
            if mode == "first":
                pres = [pq[(i * eb + j) * 8:(i * eb + j) * 8 + 8] for i in range(ea)]
                extra = back_apply(pres + scaled)
            elif mode == "second":
                extra = back_apply(scaled)
            for i in range(ea):
                terms = full[:m_rows, i * lanes:(i + 1) * lanes] * visc[i][j:j + 1]
                if mode != "first":
                    vals = jnp.concatenate(
                        [fld[(2 * j + b) * stride + 2 * i * SLOTS:
                             (2 * j + b) * stride + 2 * i * SLOTS + span] for b in range(3)], axis=0)
                    energy = energy + jnp.sum((terms * vals).reshape(m_rows // 8, 8, lanes), axis=0)
                if mode != "last":
                    add_to(out, terms + extra[:, i * lanes:(i + 1) * lanes], i, j)
                if mode == "first":
                    add_to(out2, extra[:, (ea + i) * lanes:(ea + i + 1) * lanes], i, j)
        return energy

    def collect(ref, c):
        return jnp.concatenate(
            [ref[pl.ds(a * SLOTS + c * 3 + x, nb, stride=stride), :]
             for a in range(planes) for x in range(3)], axis=0)

    def padded(part):
        return jnp.concatenate([part, jnp.zeros((width - rows, lanes), F32)], axis=0)

    def complete(fields, base):
        count = len(fields)
        span_f = slice(base, base + count)
        own_low, own_high = [], []
        for n, (even, odd, carry) in enumerate(fields):
            low = jnp.transpose(padded(even))[:8]
            high = jnp.transpose(padded(carry))[lanes - 8:]
            col_out[0, base + n] = low
            col_out[1, base + n] = high
            own_high.append(high[7:8])
        phase = 0 if base == 0 else 1
        down = remote(col_out.at[0, span_f], col_in.at[0, span_f],
                      col_send.at[phase, 0], col_recv.at[phase, 0], patch, below)
        up = remote(col_out.at[1, span_f], col_in.at[1, span_f],
                    col_send.at[phase, 1], col_recv.at[phase, 1], patch, above)

        @pl.when(has_below)
        def _():
            down.start()

        @pl.when(has_above)
        def _():
            up.start()

        @pl.when(has_above)
        def _():
            down.wait_recv()

        @pl.when(jnp.logical_not(has_above))
        def _():
            col_in[0, span_f] = jnp.zeros((count, 8, width), F32)

        @pl.when(has_below)
        def _():
            up.wait_recv()

        @pl.when(jnp.logical_not(has_below))
        def _():
            col_in[1, span_f] = jnp.zeros((count, 8, width), F32)

        halves = []
        for n, (even, odd, carry) in enumerate(fields):
            from_below = column(col_in[1, base + n][7:8])
            even = even + pltpu.roll(jnp.where(lane_n == lanes - 1, from_below, carry), 1, 1)
            ghost = jnp.where(has_above, own_high[n] + col_in[0, base + n][0:1], 0.0)
            halves.append((even, odd, ghost))
            for side, at in ((0, 0), (1, owned)):
                plane_out[side, base + n, 0] = even[at:at + block]
                plane_out[side, base + n, 1] = odd[at:at + block]
            gcol_out[base + n] = jnp.broadcast_to(ghost, (8, width))
        copies = []
        for side, to in ((0, before), (1, after)):
            copies.append(remote(plane_out.at[side, span_f], plane_in.at[side, span_f],
                                 pl_send.at[phase, side, 0], pl_recv.at[phase, side, 0], to, shell))
            copies.append(remote(gcol_out.at[span_f], gcol_in.at[side, span_f],
                                 pl_send.at[phase, side, 1], pl_recv.at[phase, side, 1], to, shell))
        for copy in copies:
            copy.start()

        @pl.when(has_below)
        def _():
            down.wait_send()

        @pl.when(has_above)
        def _():
            up.wait_send()

        for copy in copies:
            copy.wait()
        done = []
        for n, (even, odd, ghost) in enumerate(halves):
            def joined(part, k):
                return jnp.concatenate(
                    [part[:block] + plane_in[1, base + n, k], part[block:owned],
                     part[owned:] + plane_in[0, base + n, k]], axis=0)
            first = pltpu.roll(gcol_in[1, base + n], width - owned, 1)[0:1]
            last = pltpu.roll(gcol_in[0, base + n], owned, 1)[0:1]
            ghost = ghost + jnp.where(col_lane < block, first, 0.0)
            ghost = ghost + jnp.where(
                jnp.logical_and(col_lane >= owned, col_lane < rows), last, 0.0)
            done.append((joined(even, 0), joined(odd, 1), ghost))
        return done

    me = patch * n_shell + shell

    def norm_of(even, odd):
        sq = even[:owned] * even[:owned] + odd[:owned] * odd[:owned]
        return jnp.sum(sq.reshape(owned // 8, 8, lanes), axis=0)

    def sums_start(phase, norm, energy):
        sums[phase, me] = jnp.concatenate(
            [jnp.sum(norm, axis=0, keepdims=True), jnp.sum(energy, axis=0, keepdims=True)], axis=0)

        @pl.loop(1, n_dev)
        def _(d):
            to = lax.rem(me + d, n_dev)
            remote(sums.at[phase, me], sums.at[phase, me], ar_send.at[phase], ar_recv.at[phase],
                   lax.div(to, n_shell), lax.rem(to, n_shell)).start()

    def sums_end(phase):
        whole = sums.at[phase, pl.ds(0, n_dev - 1)]
        pltpu.make_async_copy(whole, whole, ar_send.at[phase]).wait()
        pltpu.make_async_copy(whole, whole, ar_recv.at[phase]).wait()
        total = jnp.sum(sums[phase], axis=0)
        total = jnp.sum(total, axis=1, keepdims=True)
        return total[0:1] / total[1:2]

    plane_copy.wait()

    @pl.when(has_below)
    def _():
        col_copy.wait_send()
        diag_copy.wait_send()

    @pl.when(has_above)
    def _():
        col_copy.wait_recv()
        diag_copy.wait_recv()

    @pl.when(jnp.logical_not(has_above))
    def _():
        vcol_in[...] = jnp.zeros_like(vcol_in)
        vdiag_in[...] = jnp.zeros_like(vdiag_in)

    v_next = exact_dot(jnp.concatenate([vplane[x] for x in range(3)], axis=0), unzip)
    v_e = jnp.concatenate([v_own[:, :lanes], v_next[:, :lanes]], axis=0)
    v_o = jnp.concatenate([v_own[:, lanes:], v_next[:, lanes:]], axis=0)
    v_g = jnp.where(col_lane < owned, vcol_in[0:1], pltpu.roll(vdiag_in[...], owned, 1)[0:1])
    put(v_e, v_o, v_g)

    operator("first", 0)
    first = (f_e - collect(out, 0), f_o - collect(out, 1), -collect(out, 2))
    second = tuple(x - collect(out2, c) for c, x in enumerate(first))
    r0, s0 = complete([first, second], 0)
    put(*r0)
    energy = operator("second", 1)
    sums_start(0, norm_of(r0[0], r0[1]), energy)
    (h0,) = complete([tuple(collect(out, c) for c in range(3))], 2)
    step0 = sums_end(0)
    r1 = tuple(s - step0 * h for s, h in zip(s0, h0))
    put(*r1)
    energy = operator("last", 2)
    sums_start(1, norm_of(r1[0], r1[1]), energy)
    part_e = (v_e + step0 * r0[0])[:owned]
    part_o = (v_o + step0 * r0[1])[:owned]
    step1 = sums_end(1)
    result = exact_dot(jnp.concatenate(
        [part_e + step1 * r1[0][:owned], part_o + step1 * r1[1][:owned]], axis=1), rezip)
    for a in range(na):
        for x in range(3):
            at = (a * 3 + x) * nb
            sol_ref[x, a] = result[at:at + nb]
    bvals[0] = 2.0 * (bvals[0] + step0 * bvals[1]) + step1 * bvals[2]
    for i in range(ea):
        for q in range(4):
            pout_ref[q, i] = p_ref[q, i] + bvals[0, pl.ds(i * eb * 8 + q, eb, stride=8), :] * inv_visc[i]


def solution(mesh):
    n_patch, n_shell = mesh.shape["patch"], mesh.shape["shell"]
    row_map = unknown_map()

    def per_device(velocity, pressure, force, viscosity, element_stiffness, element_divergence):
        ea, eb, lanes = viscosity.shape
        na, nb = velocity.shape[1], velocity.shape[2]
        dims = (n_patch, n_shell, ea, eb, na, nb, lanes)
        block = 3 * nb
        width = -(-(na + 1) * block // 128) * 128
        g_rows = (nb + 1) * (na + 1) * SLOTS
        vmem = pl.BlockSpec(memory_space=pltpu.VMEM)
        return pl.pallas_call(
            functools.partial(kernel, dims),
            out_shape=(jax.ShapeDtypeStruct(velocity.shape, F32),
                       jax.ShapeDtypeStruct(pressure.shape, F32)),
            in_specs=[vmem] * 7,
            out_specs=(vmem, vmem),
            scratch_shapes=[
                pltpu.VMEM((g_rows, lanes), F32),
                pltpu.VMEM((g_rows, lanes), BF16),
                pltpu.VMEM((g_rows, lanes), BF16),
                pltpu.VMEM((g_rows, lanes), F32),
                pltpu.VMEM((g_rows, lanes), F32),
                pltpu.VMEM((ea * eb * 8, lanes), F32),
                pltpu.VMEM((3, ea * eb * 8, lanes), F32),
                pltpu.VMEM((3, nb, 2 * lanes), F32),
                pltpu.VMEM((8, width), F32),
                pltpu.VMEM((8, width), F32),
                pltpu.VMEM((8, width), F32),
                pltpu.VMEM((2, 3, 8, width), F32),
                pltpu.VMEM((2, 3, 8, width), F32),
                pltpu.VMEM((2, 3, 2, block, lanes), F32),
                pltpu.VMEM((2, 3, 2, block, lanes), F32),
                pltpu.VMEM((3, 8, width), F32),
                pltpu.VMEM((2, 3, 8, width), F32),
                pltpu.VMEM((2, n_patch * n_shell, 2, lanes), F32),
                pltpu.SemaphoreType.DMA((3,)),
                pltpu.SemaphoreType.DMA((3,)),
                pltpu.SemaphoreType.DMA((2, 2)),
                pltpu.SemaphoreType.DMA((2, 2)),
                pltpu.SemaphoreType.DMA((2, 2, 2)),
                pltpu.SemaphoreType.DMA((2, 2, 2)),
                pltpu.SemaphoreType.DMA((2,)),
                pltpu.SemaphoreType.DMA((2,)),
            ],
            compiler_params=pltpu.CompilerParams(has_side_effects=True),
        )(velocity, pressure, force, viscosity, element_stiffness, element_divergence,
          jnp.asarray(row_map))

    spec = P(None, "patch", None, "shell")
    return jax.shard_map(
        per_device,
        mesh=mesh,
        in_specs=(spec, spec, spec, P("patch", None, "shell"), P(), P()),
        out_specs=(spec, spec),
        check_vma=False,
    )
```

time: 184 us -> 42.4 us (0.23)
  blocking collectives: 74.4 us -> 0 us
  waiting for transfers between devices: 45.1 us -> 0 us
  Pallas kernels: 0 us -> 39.4 us
  matrix products: 24.4 us -> 0 us
  starting transfers between devices: 23.3 us -> 0 us
  other arithmetic: 4.76 us -> 0 us
  local copies, waits for them, and re-layouts: 6.08 us -> 2.24 us
  between operations: 4.05 us -> 0.65 us
    psum x2 -> x0, blocking collectives: 74.4 us -> none  [per_device(): norm_sq = lax.psum(local_norm, ('patch', 'shell'))]
    ppermute x14 -> x0, waiting for transfers between devices: 45.1 us -> none  [the longest x7 36 us: from_behind(): return lax.ppermute(value, axis, pairs)]
    pallas_call x0 -> x1, Pallas kernels: none -> 39.4 us  [per_device(): pl.pallas_call(functools.partial(kernel, dims), out_shape=(jax.ShapeDtype...]
    dot_general x35 -> x0, matrix products: 24.4 us -> none  [the longest x5 4.06 us: element_values(): jnp.einsum('xpbcjk,api->xabcijk', middle, sel_a, precision=lax.Precision....]
    ppermute x14 -> x0, starting transfers between devices: 23.3 us -> none  [the longest x7 11.8 us: passed_along(): return lax.ppermute(block, axis, route)]
    unnamed x23 -> x4, local copies, waits for them, and re-layouts: 3.69 us -> 2.24 us
  transfers between devices with their start and end apart: 14 -> 0, of which waited for: 14 -> 0; matrix products, arithmetic and copies ran while one was open for 1% -> 0% of each run, Pallas kernels for 0% -> 0%
where the time goes in v1:
time: 42.4 us; the launch traced here: 42.3 us
  Pallas kernels  39.4 us (93%)
  local copies, waits for them, and re-layouts  2.24 us (5%)
  between operations  0.65 us (2%)
    pallas_call x1, Pallas kernels, per_device(): pl.pallas_call(functools.partial(kernel, dims), out_shape=(jax.ShapeDtype...  39.4 us
    unnamed x4, local copies, waits for them, and re-layouts  2.24 us

profile of v1, /device:TPU:0, one launch (start us, length us, event | category | flops | bytes accessed | tf_op | source)
XLA Modules:
  0.0 42.3 jit_solution(313342268820591045)
XLA Ops:
  0.6 39.4 %shard_map.86 = (f32[3,4,16,256]{3,2,1,0:T(8,128)}, f32[4,2,8,128]{3,2,1,0:T(8,128)}) custom-call(f32[3,4,16,256]{3,2,1,0:T(8,128)} %v_ref.1, f32[4,2,8,128]{3,2,1,0:T(8,128)} %p_ref.1, f32[3,4,16,256]{3,2,1,0:T(8,128)} %f_ref.1, f32[2,8,128]{2,1,0:T(8,128)} %visc_ref.1, f32[81,81]{1,0:T(8,128)} %stiff_ref.1, f32[4,81]{1,0:T(4,128)} %div_ref.1, ...), custom_call_target="tpu_custom_call" | custom-call | tf_op jit(solution)/shard_map/pallas_call | solution.py:379
  40.0 0.0 copy-start
  40.0 1.6 %copy.11 = f32[3,4,16,256]{3,2,1,0:T(8,128)} copy(f32[3,4,16,256]{3,2,1,0:T(8,128)} %get-tuple-element.4) | data formatting | bytes 393216
  41.6 0.0 copy-done
  41.6 0.6 %copy.12 = f32[4,2,8,128]{3,2,1,0:T(8,128)} copy(f32[4,2,8,128]{3,2,1,0:T(8,128)S(1)} %copy-done) | data formatting | bytes 65536
Async XLA Ops:
  40.0 1.6 %copy-start = (f32[4,2,8,128]{3,2,1,0:T(8,128)S(1)}, f32[4,2,8,128]{3,2,1,0:T(8,128)}, u32[]{:S(2)}) copy-start(f32[4,2,8,128]{3,2,1,0:T(8,128)} %get-tuple-element.5) | copy-start | bytes 98308

commit v2 on v1

--- a/solution.py
+++ b/solution.py
@@ -42,12 +42,13 @@
 
 def kernel(
     dims,
-    v_ref, p_ref, f_ref, visc_ref, stiff_ref, div_ref, map_ref,
+    v_hbm, p_hbm, f_hbm, visc_hbm, stiff_hbm, div_hbm, map_hbm,
     sol_ref, pout_ref,
+    v_ref, p_ref, f_ref, visc_ref, stiff_ref, div_ref, map_ref, in_sems,
     fld, fhi, flo, out, out2, pq, bvals,
     vplane, vcol, vcol_in, vdiag_in,
-    col_out, col_in, plane_out, plane_in, gcol_out, gcol_in, sums,
-    bar_send, bar_recv, col_send, col_recv, pl_send, pl_recv, ar_send, ar_recv,
+    col_out, col_in, plane_out, plane_in, sums,
+    bar_send, bar_recv, ex_send, ex_recv, ar_send, ar_recv,
 ):
     n_patch, n_shell, ea, eb, na, nb, lanes = dims
     n_dev = n_patch * n_shell
@@ -72,19 +73,46 @@
             device_id={"patch": to_patch, "shell": to_shell}, device_id_type=MESH,
         )
 
-    plane_copy = remote(v_ref.at[:, 0], vplane, bar_send.at[0], bar_recv.at[0], before, shell)
-    plane_copy.start()
+    loads = [
+        pltpu.make_async_copy(source, target, in_sems.at[k])
+        for k, (source, target) in enumerate((
+            (v_hbm, v_ref), (stiff_hbm, stiff_ref), (div_hbm, div_ref), (map_hbm, map_ref),
+            (f_hbm, f_ref), (p_hbm, p_ref), (visc_hbm, visc_ref)))
+    ]
+    for load in loads:
+        load.start()
+    barrier = pltpu.get_barrier_semaphore()
+
+    @pl.loop(1, n_dev)
+    def _(d):
+        to = lax.rem(patch * n_shell + shell + d, n_dev)
+        pl.semaphore_signal(
+            barrier, inc=1, device_id_type=MESH,
+            device_id={"patch": lax.div(to, n_shell), "shell": lax.rem(to, n_shell)})
+
+    @pl.when(jnp.logical_not(has_above))
+    def _():
+        col_in[2] = jnp.zeros(col_in.shape[1:], F32)
+        vcol_in[...] = jnp.zeros_like(vcol_in)
+        vdiag_in[...] = jnp.zeros_like(vdiag_in)
+
+    @pl.when(jnp.logical_not(has_below))
+    def _():
+        col_in[1] = jnp.zeros(col_in.shape[1:], F32)
+
+    fld[...] = jnp.zeros_like(fld)
+    pq[...] = jnp.zeros_like(pq)
+    out[...] = jnp.zeros_like(out)
+    out2[...] = jnp.zeros_like(out2)
+    for load in loads:
+        load.wait()
+    plane_copy = remote(v_hbm.at[:, 0], vplane, bar_send.at[0], bar_recv.at[0], before, shell)
     head = jnp.concatenate(
         [v_ref[x, a, :, :lanes] for a in range(na) for x in range(3)]
         + [jnp.zeros((width - owned, lanes), F32)], axis=0)
     vcol[...] = jnp.transpose(head)[:8]
     col_copy = remote(vcol, vcol_in, bar_send.at[1], bar_recv.at[1], patch, below)
     diag_copy = remote(vcol, vdiag_in, bar_send.at[2], bar_recv.at[2], before, below)
-
-    @pl.when(has_below)
-    def _():
-        col_copy.start()
-        diag_copy.start()
 
     row_map = map_ref[...].astype(BF16)
     a_hi, a_lo = split2(stiff_ref[...])
@@ -111,8 +139,6 @@
     unzip = (r_i == jnp.where(c_i < lanes, 2 * c_i, 2 * c_i - 2 * lanes + 1)).astype(BF16)
     rezip = (c_i == jnp.where(r_i < lanes, 2 * r_i, 2 * r_i - 2 * lanes + 1)).astype(BF16)
 
-    fld[...] = jnp.zeros_like(fld)
-    pq[...] = jnp.zeros_like(pq)
     for i in range(ea):
         for q in range(4):
             pq[pl.ds(i * eb * 8 + q, eb, stride=8), :] = p_ref[q, i]
@@ -126,6 +152,14 @@
     f_o = jnp.concatenate([f_n[:, lanes:], zero_plane], axis=0)
     v_own = exact_dot(jnp.concatenate(
         [v_ref[x, a] for a in range(na) for x in range(3)], axis=0), unzip)
+
+    pl.semaphore_wait(barrier, n_dev - 1)
+    plane_copy.start()
+
+    @pl.when(has_below)
+    def _():
+        col_copy.start()
+        diag_copy.start()
 
     lane_n = lax.broadcasted_iota(jnp.int32, (rows, lanes), 1)
     col_lane = lax.broadcasted_iota(jnp.int32, (1, width), 1)
@@ -165,28 +199,31 @@
             ref[at:at + span] = ref[at:at + span] + terms[b * span:(b + 1) * span]
 
     def operator(mode, slot):
-        if mode != "last":
+        if mode == "second":
             out[...] = jnp.zeros_like(out)
-        if mode == "first":
-            out2[...] = jnp.zeros_like(out2)
         energy = jnp.zeros((8, lanes), F32)
-        for j in range(eb):
-            hi = dot(apply_all, gathered(fhi, j))
-            full = hi[:m_rows + 8] + hi[m_rows + 8:] + dot(apply_hi, gathered(flo, j))
+        full = None
+        for step in range(eb + 1):
+            ready = full
+            if step < eb:
+                hi = dot(apply_all, gathered(fhi, step))
+                full = hi[:m_rows + 8] + hi[m_rows + 8:] + dot(apply_hi, gathered(flo, step))
+            if step == 0:
+                continue
+            j = step - 1
             scaled = []
             for i in range(ea):
-                part = full[:, i * lanes:(i + 1) * lanes]
+                bv = ready[m_rows:, i * lanes:(i + 1) * lanes]
                 at = (i * eb + j) * 8
-                bv = part[m_rows:]
                 bvals[slot, at:at + 8] = bv
-                scaled.append(bv * inv_visc[i][j:j + 1])
-            if mode == "first":
-                pres = [pq[(i * eb + j) * 8:(i * eb + j) * 8 + 8] for i in range(ea)]
-                extra = back_apply(pres + scaled)
-            elif mode == "second":
+                if mode == "first":
+                    scaled.append(pq[at:at + 8])
+                else:
+                    scaled.append(bv * inv_visc[i][j:j + 1])
+            if mode != "last":
                 extra = back_apply(scaled)
             for i in range(ea):
-                terms = full[:m_rows, i * lanes:(i + 1) * lanes] * visc[i][j:j + 1]
+                terms = ready[:m_rows, i * lanes:(i + 1) * lanes] * visc[i][j:j + 1]
                 if mode != "first":
                     vals = jnp.concatenate(
                         [fld[(2 * j + b) * stride + 2 * i * SLOTS:
@@ -194,9 +231,15 @@
                     energy = energy + jnp.sum((terms * vals).reshape(m_rows // 8, 8, lanes), axis=0)
                 if mode != "last":
                     add_to(out, terms + extra[:, i * lanes:(i + 1) * lanes], i, j)
-                if mode == "first":
-                    add_to(out2, extra[:, (ea + i) * lanes:(ea + i + 1) * lanes], i, j)
         return energy
+
+    def pressure_change():
+        for j in range(eb):
+            extra = back_apply(
+                [bvals[0, (i * eb + j) * 8:(i * eb + j) * 8 + 8] * inv_visc[i][j:j + 1]
+                 for i in range(ea)])
+            for i in range(ea):
+                add_to(out2, extra[:, i * lanes:(i + 1) * lanes], i, j)
 
     def collect(ref, c):
         return jnp.concatenate(
@@ -206,88 +249,82 @@
     def padded(part):
         return jnp.concatenate([part, jnp.zeros((width - rows, lanes), F32)], axis=0)
 
-    def complete(fields, base):
-        count = len(fields)
-        span_f = slice(base, base + count)
-        own_low, own_high = [], []
-        for n, (even, odd, carry) in enumerate(fields):
-            low = jnp.transpose(padded(even))[:8]
-            high = jnp.transpose(padded(carry))[lanes - 8:]
-            col_out[0, base + n] = low
-            col_out[1, base + n] = high
-            own_high.append(high[7:8])
-        phase = 0 if base == 0 else 1
-        down = remote(col_out.at[0, span_f], col_in.at[0, span_f],
-                      col_send.at[phase, 0], col_recv.at[phase, 0], patch, below)
-        up = remote(col_out.at[1, span_f], col_in.at[1, span_f],
-                    col_send.at[phase, 1], col_recv.at[phase, 1], patch, above)
+    def stage(n, even, odd, carry):
+        even = even + pltpu.roll(jnp.where(lane_n == lanes - 1, 0.0, carry), 1, 1)
+        high = jnp.transpose(padded(carry))[lanes - 8:][7:8]
+        col_out[0, n] = high
+        col_out[1, n] = jnp.transpose(padded(even))[:8][0:1]
+        for side, at in ((0, 0), (1, owned)):
+            plane_out[side, n, 0] = even[at:at + block]
+            plane_out[side, n, 1] = odd[at:at + block]
+        flat, up, down = [], [], []
+
+        def message(group, source, target, k, to_patch, to_shell):
+            group.append(remote(source, target, ex_send.at[n, k], ex_recv.at[n, k],
+                                to_patch, to_shell))
+
+        message(flat, plane_out.at[0, n], plane_in.at[0, n], 0, before, shell)
+        message(flat, plane_out.at[1, n], plane_in.at[1, n], 1, after, shell)
+        for src, to in ((1, after), (2, before)):
+            message(flat, col_out.at[0, n], col_in.at[0, n, src], 1 + src, to, shell)
+        for src, to in ((0, patch), (1, after), (2, before)):
+            message(up, col_out.at[0, n], col_in.at[1, n, src], 4 + src, to, above)
+            message(down, col_out.at[1, n], col_in.at[2, n, src], 7 + src, to, below)
+        return even, odd, high, (flat, up, down)
+
+    def begin(staged):
+        flat, up, down = staged[3]
+
+        @pl.when(has_above)
+        def _():
+            for copy in up:
+                copy.start()
 
         @pl.when(has_below)
         def _():
-            down.start()
+            for copy in down:
+                copy.start()
+
+        for copy in flat[2:] + flat[:2]:
+            copy.start()
+
+    def complete(n, staged):
+        even, odd, high, (flat, up, down) = staged
 
         @pl.when(has_above)
         def _():
-            up.start()
-
-        @pl.when(has_above)
-        def _():
-            down.wait_recv()
-
-        @pl.when(jnp.logical_not(has_above))
-        def _():
-            col_in[0, span_f] = jnp.zeros((count, 8, width), F32)
+            for copy in down:
+                copy.wait_recv()
+            for copy in up:
+                copy.wait_send()
 
         @pl.when(has_below)
         def _():
-            up.wait_recv()
-
-        @pl.when(jnp.logical_not(has_below))
-        def _():
-            col_in[1, span_f] = jnp.zeros((count, 8, width), F32)
-
-        halves = []
-        for n, (even, odd, carry) in enumerate(fields):
-            from_below = column(col_in[1, base + n][7:8])
-            even = even + pltpu.roll(jnp.where(lane_n == lanes - 1, from_below, carry), 1, 1)
-            ghost = jnp.where(has_above, own_high[n] + col_in[0, base + n][0:1], 0.0)
-            halves.append((even, odd, ghost))
-            for side, at in ((0, 0), (1, owned)):
-                plane_out[side, base + n, 0] = even[at:at + block]
-                plane_out[side, base + n, 1] = odd[at:at + block]
-            gcol_out[base + n] = jnp.broadcast_to(ghost, (8, width))
-        copies = []
-        for side, to in ((0, before), (1, after)):
-            copies.append(remote(plane_out.at[side, span_f], plane_in.at[side, span_f],
-                                 pl_send.at[phase, side, 0], pl_recv.at[phase, side, 0], to, shell))
-            copies.append(remote(gcol_out.at[span_f], gcol_in.at[side, span_f],
-                                 pl_send.at[phase, side, 1], pl_recv.at[phase, side, 1], to, shell))
-        for copy in copies:
-            copy.start()
-
-        @pl.when(has_below)
-        def _():
-            down.wait_send()
-
-        @pl.when(has_above)
-        def _():
-            up.wait_send()
-
-        for copy in copies:
+            for copy in up:
+                copy.wait_recv()
+            for copy in down:
+                copy.wait_send()
+
+        for copy in flat:
             copy.wait()
-        done = []
-        for n, (even, odd, ghost) in enumerate(halves):
-            def joined(part, k):
-                return jnp.concatenate(
-                    [part[:block] + plane_in[1, base + n, k], part[block:owned],
-                     part[owned:] + plane_in[0, base + n, k]], axis=0)
-            first = pltpu.roll(gcol_in[1, base + n], width - owned, 1)[0:1]
-            last = pltpu.roll(gcol_in[0, base + n], owned, 1)[0:1]
-            ghost = ghost + jnp.where(col_lane < block, first, 0.0)
-            ghost = ghost + jnp.where(
-                jnp.logical_and(col_lane >= owned, col_lane < rows), last, 0.0)
-            done.append((joined(even, 0), joined(odd, 1), ghost))
-        return done
+
+        def joined_row(own, kind):
+            prev = jnp.broadcast_to(col_in[kind, n, 1], (8, width))
+            nxt = jnp.broadcast_to(col_in[kind, n, 2], (8, width))
+            row = own + jnp.where(col_lane < block, pltpu.roll(prev, width - owned, 1)[0:1], 0.0)
+            return row + jnp.where(
+                jnp.logical_and(col_lane >= owned, col_lane < rows),
+                pltpu.roll(nxt, owned, 1)[0:1], 0.0)
+
+        def joined(part, k):
+            return jnp.concatenate(
+                [part[:block] + plane_in[1, n, k], part[block:owned],
+                 part[owned:] + plane_in[0, n, k]], axis=0)
+
+        ghost = jnp.where(
+            has_above, joined_row(high, 0) + joined_row(col_in[2, n, 0], 2), 0.0)
+        from_below = column(joined_row(col_in[1, n, 0], 1))
+        return (joined(even, 0) + jnp.where(lane_n == 0, from_below, 0.0), joined(odd, 1), ghost)
 
     me = patch * n_shell + shell
 
@@ -325,11 +362,6 @@
         col_copy.wait_recv()
         diag_copy.wait_recv()
 
-    @pl.when(jnp.logical_not(has_above))
-    def _():
-        vcol_in[...] = jnp.zeros_like(vcol_in)
-        vdiag_in[...] = jnp.zeros_like(vdiag_in)
-
     v_next = exact_dot(jnp.concatenate([vplane[x] for x in range(3)], axis=0), unzip)
     v_e = jnp.concatenate([v_own[:, :lanes], v_next[:, :lanes]], axis=0)
     v_o = jnp.concatenate([v_own[:, lanes:], v_next[:, lanes:]], axis=0)
@@ -337,15 +369,22 @@
     put(v_e, v_o, v_g)
 
     operator("first", 0)
-    first = (f_e - collect(out, 0), f_o - collect(out, 1), -collect(out, 2))
-    second = tuple(x - collect(out2, c) for c, x in enumerate(first))
-    r0, s0 = complete([first, second], 0)
+    sent = stage(0, f_e - collect(out, 0), f_o - collect(out, 1), -collect(out, 2))
+    begin(sent)
+    pressure_change()
+    sent_change = stage(1, *[collect(out2, c) for c in range(3)])
+    r0 = complete(0, sent)
+    begin(sent_change)
     put(*r0)
     energy = operator("second", 1)
     sums_start(0, norm_of(r0[0], r0[1]), energy)
-    (h0,) = complete([tuple(collect(out, c) for c in range(3))], 2)
+    sent = stage(2, *[collect(out, c) for c in range(3)])
+    begin(sent)
+    change = complete(1, sent_change)
+    base = [x - y for x, y in zip(r0, change)]
+    h0 = complete(2, sent)
     step0 = sums_end(0)
-    r1 = tuple(s - step0 * h for s, h in zip(s0, h0))
+    r1 = tuple(s - step0 * h for s, h in zip(base, h0))
     put(*r1)
     energy = operator("last", 2)
     sums_start(1, norm_of(r1[0], r1[1]), energy)
@@ -380,9 +419,17 @@
             functools.partial(kernel, dims),
             out_shape=(jax.ShapeDtypeStruct(velocity.shape, F32),
                        jax.ShapeDtypeStruct(pressure.shape, F32)),
-            in_specs=[vmem] * 7,
+            in_specs=[pl.BlockSpec(memory_space=pl.ANY)] * 7,
             out_specs=(vmem, vmem),
             scratch_shapes=[
+                pltpu.VMEM(velocity.shape, F32),
+                pltpu.VMEM(pressure.shape, F32),
+                pltpu.VMEM(force.shape, F32),
+                pltpu.VMEM(viscosity.shape, F32),
+                pltpu.VMEM(element_stiffness.shape, F32),
+                pltpu.VMEM(element_divergence.shape, F32),
+                pltpu.VMEM(row_map.shape, F32),
+                pltpu.SemaphoreType.DMA((7,)),
                 pltpu.VMEM((g_rows, lanes), F32),
                 pltpu.VMEM((g_rows, lanes), BF16),
                 pltpu.VMEM((g_rows, lanes), BF16),
@@ -394,23 +441,19 @@
                 pltpu.VMEM((8, width), F32),
                 pltpu.VMEM((8, width), F32),
                 pltpu.VMEM((8, width), F32),
-                pltpu.VMEM((2, 3, 8, width), F32),
-                pltpu.VMEM((2, 3, 8, width), F32),
+                pltpu.VMEM((2, 3, 1, width), F32),
+                pltpu.VMEM((3, 3, 3, 1, width), F32),
                 pltpu.VMEM((2, 3, 2, block, lanes), F32),
                 pltpu.VMEM((2, 3, 2, block, lanes), F32),
-                pltpu.VMEM((3, 8, width), F32),
-                pltpu.VMEM((2, 3, 8, width), F32),
                 pltpu.VMEM((2, n_patch * n_shell, 2, lanes), F32),
                 pltpu.SemaphoreType.DMA((3,)),
                 pltpu.SemaphoreType.DMA((3,)),
-                pltpu.SemaphoreType.DMA((2, 2)),
-                pltpu.SemaphoreType.DMA((2, 2)),
-                pltpu.SemaphoreType.DMA((2, 2, 2)),
-                pltpu.SemaphoreType.DMA((2, 2, 2)),
+                pltpu.SemaphoreType.DMA((3, 10)),
+                pltpu.SemaphoreType.DMA((3, 10)),
                 pltpu.SemaphoreType.DMA((2,)),
                 pltpu.SemaphoreType.DMA((2,)),
             ],
-            compiler_params=pltpu.CompilerParams(has_side_effects=True),
+            compiler_params=pltpu.CompilerParams(collective_id=0, has_side_effects=True),
         )(velocity, pressure, force, viscosity, element_stiffness, element_divergence,
           jnp.asarray(row_map))
 

time: 42.4 us -> 36 us (0.85)
  Pallas kernels: 39.4 us -> 32.9 us
    pallas_call x1, Pallas kernels: 39.4 us -> 32.9 us  [per_device(): pl.pallas_call(functools.partial(kernel, dims), out_shape=(jax.ShapeDtype...]
where the time goes in v2:
time: 36 us; the launch traced here: 35.8 us
  Pallas kernels  32.9 us (91%)
  local copies, waits for them, and re-layouts  2.24 us (6%)
  between operations  0.65 us (2%)
    pallas_call x1, Pallas kernels, per_device(): pl.pallas_call(functools.partial(kernel, dims), out_shape=(jax.ShapeDtype...  32.9 us
    unnamed x4, local copies, waits for them, and re-layouts  2.24 us

profile of v2, /device:TPU:0, one launch (start us, length us, event | category | flops | bytes accessed | tf_op | source)
XLA Modules:
  0.0 35.8 jit_solution(4207188182712033067)
XLA Ops:
  0.6 32.9 %shard_map.86 = (f32[3,4,16,256]{3,2,1,0:T(8,128)}, f32[4,2,8,128]{3,2,1,0:T(8,128)}) custom-call(f32[3,4,16,256]{3,2,1,0:T(8,128)} %v_hbm.1, f32[4,2,8,128]{3,2,1,0:T(8,128)} %p_hbm.1, f32[3,4,16,256]{3,2,1,0:T(8,128)} %f_hbm.1, f32[2,8,128]{2,1,0:T(8,128)} %visc_hbm.1, f32[81,81]{1,0:T(8,128)} %stiff_hbm.1, f32[4,81]{1,0:T(4,128)} %div_hbm.1, ...), custom_call_target="tpu_custom_call" | custom-call | tf_op jit(solution)/shard_map/pallas_call | solution.py:418
  33.6 0.0 copy-start
  33.6 1.6 %copy.11 = f32[3,4,16,256]{3,2,1,0:T(8,128)} copy(f32[3,4,16,256]{3,2,1,0:T(8,128)} %get-tuple-element.4) | data formatting | bytes 393216
  35.2 0.0 copy-done
  35.2 0.6 %copy.12 = f32[4,2,8,128]{3,2,1,0:T(8,128)} copy(f32[4,2,8,128]{3,2,1,0:T(8,128)S(1)} %copy-done) | data formatting | bytes 65536
Async XLA Ops:
  33.6 1.6 %copy-start = (f32[4,2,8,128]{3,2,1,0:T(8,128)S(1)}, f32[4,2,8,128]{3,2,1,0:T(8,128)}, u32[]{:S(2)}) copy-start(f32[4,2,8,128]{3,2,1,0:T(8,128)} %get-tuple-element.5) | copy-start | bytes 98308

commit v3 on v2

--- a/solution.py
+++ b/solution.py
@@ -47,7 +47,7 @@
     v_ref, p_ref, f_ref, visc_ref, stiff_ref, div_ref, map_ref, in_sems,
     fld, fhi, flo, out, out2, pq, bvals,
     vplane, vcol, vcol_in, vdiag_in,
-    col_out, col_in, plane_out, plane_in, sums,
+    col_out, col_in, plane_out, plane_in, sums, far_sums,
     bar_send, bar_recv, ex_send, ex_recv, ar_send, ar_recv,
 ):
     n_patch, n_shell, ea, eb, na, nb, lanes = dims
@@ -326,28 +326,45 @@
         from_below = column(joined_row(col_in[1, n, 0], 1))
         return (joined(even, 0) + jnp.where(lane_n == 0, from_below, 0.0), joined(odd, 1), ghost)
 
-    me = patch * n_shell + shell
+    inner = max(k for k in range(1, n_patch + 1) if k * k <= n_patch and n_patch % k == 0)
+    n_near, n_far = inner * n_shell, n_patch // inner
+    group = lax.div(patch, inner)
+    near = lax.rem(patch, inner) * n_shell + shell
 
     def norm_of(even, odd):
         sq = even[:owned] * even[:owned] + odd[:owned] * odd[:owned]
         return jnp.sum(sq.reshape(owned // 8, 8, lanes), axis=0)
 
     def sums_start(phase, norm, energy):
-        sums[phase, me] = jnp.concatenate(
+        sums[phase, near] = jnp.concatenate(
             [jnp.sum(norm, axis=0, keepdims=True), jnp.sum(energy, axis=0, keepdims=True)], axis=0)
 
-        @pl.loop(1, n_dev)
+        @pl.loop(1, n_near)
         def _(d):
-            to = lax.rem(me + d, n_dev)
-            remote(sums.at[phase, me], sums.at[phase, me], ar_send.at[phase], ar_recv.at[phase],
-                   lax.div(to, n_shell), lax.rem(to, n_shell)).start()
+            to = lax.rem(near + d, n_near)
+            remote(sums.at[phase, near], sums.at[phase, near],
+                   ar_send.at[phase, 0], ar_recv.at[phase, 0],
+                   group * inner + lax.div(to, n_shell), lax.rem(to, n_shell)).start()
+
+    def settle(buffer, count, phase, level):
+        if count > 1:
+            whole = buffer.at[phase, pl.ds(0, count - 1)]
+            pltpu.make_async_copy(whole, whole, ar_send.at[phase, level]).wait()
+            pltpu.make_async_copy(whole, whole, ar_recv.at[phase, level]).wait()
+        return jnp.sum(buffer[phase], axis=0)
+
+    def sums_middle(phase):
+        far_sums[phase, group] = settle(sums, n_near, phase, 0)
+
+        @pl.loop(1, n_far)
+        def _(d):
+            to = lax.rem(group + d, n_far)
+            remote(far_sums.at[phase, group], far_sums.at[phase, group],
+                   ar_send.at[phase, 1], ar_recv.at[phase, 1],
+                   to * inner + lax.rem(patch, inner), shell).start()
 
     def sums_end(phase):
-        whole = sums.at[phase, pl.ds(0, n_dev - 1)]
-        pltpu.make_async_copy(whole, whole, ar_send.at[phase]).wait()
-        pltpu.make_async_copy(whole, whole, ar_recv.at[phase]).wait()
-        total = jnp.sum(sums[phase], axis=0)
-        total = jnp.sum(total, axis=1, keepdims=True)
+        total = jnp.sum(settle(far_sums, n_far, phase, 1), axis=1, keepdims=True)
         return total[0:1] / total[1:2]
 
     plane_copy.wait()
@@ -382,6 +399,7 @@
     begin(sent)
     change = complete(1, sent_change)
     base = [x - y for x, y in zip(r0, change)]
+    sums_middle(0)
     h0 = complete(2, sent)
     step0 = sums_end(0)
     r1 = tuple(s - step0 * h for s, h in zip(base, h0))
@@ -390,6 +408,7 @@
     sums_start(1, norm_of(r1[0], r1[1]), energy)
     part_e = (v_e + step0 * r0[0])[:owned]
     part_o = (v_o + step0 * r0[1])[:owned]
+    sums_middle(1)
     step1 = sums_end(1)
     result = exact_dot(jnp.concatenate(
         [part_e + step1 * r1[0][:owned], part_o + step1 * r1[1][:owned]], axis=1), rezip)
@@ -406,6 +425,7 @@
 def solution(mesh):
     n_patch, n_shell = mesh.shape["patch"], mesh.shape["shell"]
     row_map = unknown_map()
+    inner = max(k for k in range(1, n_patch + 1) if k * k <= n_patch and n_patch % k == 0)
 
     def per_device(velocity, pressure, force, viscosity, element_stiffness, element_divergence):
         ea, eb, lanes = viscosity.shape
@@ -445,13 +465,14 @@
                 pltpu.VMEM((3, 3, 3, 1, width), F32),
                 pltpu.VMEM((2, 3, 2, block, lanes), F32),
                 pltpu.VMEM((2, 3, 2, block, lanes), F32),
-                pltpu.VMEM((2, n_patch * n_shell, 2, lanes), F32),
+                pltpu.VMEM((2, inner * n_shell, 2, lanes), F32),
+                pltpu.VMEM((2, n_patch // inner, 2, lanes), F32),
                 pltpu.SemaphoreType.DMA((3,)),
                 pltpu.SemaphoreType.DMA((3,)),
                 pltpu.SemaphoreType.DMA((3, 10)),
                 pltpu.SemaphoreType.DMA((3, 10)),
-                pltpu.SemaphoreType.DMA((2,)),
-                pltpu.SemaphoreType.DMA((2,)),
+                pltpu.SemaphoreType.DMA((2, 2)),
+                pltpu.SemaphoreType.DMA((2, 2)),
             ],
             compiler_params=pltpu.CompilerParams(collective_id=0, has_side_effects=True),
         )(velocity, pressure, force, viscosity, element_stiffness, element_divergence,

time: 36 us -> 39.2 us (1.089)
  Pallas kernels: 32.9 us -> 36.1 us
    pallas_call x1, Pallas kernels: 32.9 us -> 36.1 us  [per_device(): pl.pallas_call(functools.partial(kernel, dims), out_shape=(jax.ShapeDtype...]
where the time goes in v3:
time: 39.2 us; the launch traced here: 39 us
  Pallas kernels  36.1 us (92%)
  local copies, waits for them, and re-layouts  2.24 us (6%)
  between operations  0.65 us (2%)
    pallas_call x1, Pallas kernels, per_device(): pl.pallas_call(functools.partial(kernel, dims), out_shape=(jax.ShapeDtype...  36.1 us
    unnamed x4, local copies, waits for them, and re-layouts  2.24 us

profile of v3, /device:TPU:0, one launch (start us, length us, event | category | flops | bytes accessed | tf_op | source)
XLA Modules:
  0.0 39.0 jit_solution(5075357464773194935)
XLA Ops:
  0.6 36.1 %shard_map.86 = (f32[3,4,16,256]{3,2,1,0:T(8,128)}, f32[4,2,8,128]{3,2,1,0:T(8,128)}) custom-call(f32[3,4,16,256]{3,2,1,0:T(8,128)} %v_hbm.1, f32[4,2,8,128]{3,2,1,0:T(8,128)} %p_hbm.1, f32[3,4,16,256]{3,2,1,0:T(8,128)} %f_hbm.1, f32[2,8,128]{2,1,0:T(8,128)} %visc_hbm.1, f32[81,81]{1,0:T(8,128)} %stiff_hbm.1, f32[4,81]{1,0:T(4,128)} %div_hbm.1, ...), custom_call_target="tpu_custom_call" | custom-call | tf_op jit(solution)/shard_map/pallas_call | solution.py:438
  36.7 0.0 copy-start
  36.8 1.6 %copy.11 = f32[3,4,16,256]{3,2,1,0:T(8,128)} copy(f32[3,4,16,256]{3,2,1,0:T(8,128)} %get-tuple-element.4) | data formatting | bytes 393216
  38.4 0.0 copy-done
  38.4 0.6 %copy.12 = f32[4,2,8,128]{3,2,1,0:T(8,128)} copy(f32[4,2,8,128]{3,2,1,0:T(8,128)S(1)} %copy-done) | data formatting | bytes 65536
Async XLA Ops:
  36.7 1.6 %copy-start = (f32[4,2,8,128]{3,2,1,0:T(8,128)S(1)}, f32[4,2,8,128]{3,2,1,0:T(8,128)}, u32[]{:S(2)}) copy-start(f32[4,2,8,128]{3,2,1,0:T(8,128)} %get-tuple-element.5) | copy-start | bytes 98308
